TPU v7x, 8 devices: a whole 2x2x1 slice. The times are simulated.
8 devices in a mesh: dp: 2 (over z, y), tp: 4 (over x, core).
Axes of the slice: x: 2, y: 2, z: 1, core: 2. Of those that a mesh axis runs over, the one named last changes fastest.
Arguments:
- hidden: bfloat16 [2, 256, 5120], P('dp', 'tp'), parts along dimension 0
- attn_gain: float32 [5120], replicated
- attn_bias: float32 [5120], replicated
- mlp_gain: float32 [5120], replicated
- mlp_bias: float32 [5120], replicated
- w_qkv: bfloat16 [5120, 40, 384], P(None, 'tp')
- w_out: bfloat16 [5120, 5120], P('tp')
- w_up: bfloat16 [5120, 20480], P(None, 'tp')
- w_down: bfloat16 [20480, 5120], P('tp')
- positions: int32 [256], replicated
Outputs:
- output: bfloat16 [2, 256, 5120], P('dp', 'tp'), parts along dimension 0
There are 2 independent parts. A program takes and returns all parts, laid end to end along the dimension named above; an argument that names none is the same for every part.
All inputs are finite; a program needn't handle non-finite values.
Results may differ from a plain program's by a relative error of at most 0.00364416.
Values are sent between devices in bfloat16 or wider.
A program may use at most 1 GiB of HBM per device.

v0:
```python
import jax
import jax.numpy as jnp
from jax import lax
from jax.sharding import PartitionSpec as P


def layer_norm(tok_rows, norm_gain, norm_bias):
    rows32 = tok_rows.astype(jnp.float32)
    row_mean = jnp.mean(rows32, axis=-1, keepdims=True)
    centered = rows32 - row_mean
    row_var = jnp.mean(centered * centered, axis=-1, keepdims=True)
    return (centered * lax.rsqrt(row_var + 1e-5) * norm_gain + norm_bias).astype(jnp.bfloat16)


def rotary_tables(positions, head_dim):
    inv_freq = 10000.0 ** (-2.0 * jnp.arange(head_dim // 2, dtype=jnp.float32) / head_dim)
    angles = positions.astype(jnp.float32)[:, None] * inv_freq[None, :]
    angles = jnp.concatenate([angles, angles], axis=-1)
    return jnp.cos(angles), jnp.sin(angles)


def apply_rotary(head_vals, cos_tab, sin_tab):
    half_dim = head_vals.shape[-1] // 2
    vals32 = head_vals.astype(jnp.float32)
    rotated = jnp.concatenate([-vals32[..., half_dim:], vals32[..., :half_dim]], axis=-1)
    return (vals32 * cos_tab + rotated * sin_tab).astype(jnp.bfloat16)


def attention_branch(normed, w_qkv_part, w_out_part, positions):
    batch_size, seq_len, model_width = normed.shape
    num_groups = w_qkv_part.shape[1]
    slot_cols = w_qkv_part.shape[2]
    group_cols = w_out_part.shape[0] // num_groups
    head_dim = (slot_cols - group_cols) // 2
    group_size = group_cols // head_dim
    qkv_rows = jnp.einsum('bsd,dkc->bskc', normed, w_qkv_part, preferred_element_type=jnp.float32).astype(jnp.bfloat16)
    qkv_rows = qkv_rows.reshape(batch_size, seq_len, num_groups, group_size + 2, head_dim)
    cos_tab, sin_tab = rotary_tables(positions, head_dim)
    query_rot = apply_rotary(qkv_rows[:, :, :, :group_size, :], cos_tab[None, :, None, None, :], sin_tab[None, :, None, None, :])
    key_rot = apply_rotary(qkv_rows[:, :, :, group_size, :], cos_tab[None, :, None, :], sin_tab[None, :, None, :])
    value_seq = qkv_rows[:, :, :, group_size + 1, :]
    block_len = min(seq_len, 256)
    num_blocks = seq_len // block_len
    key_idx = jnp.arange(seq_len)
    score_scale = head_dim ** -0.5

    def one_block(block_idx):
        row_start = block_idx * block_len
        query_blk = lax.dynamic_slice_in_dim(query_rot, row_start, block_len, axis=1)
        scores = jnp.einsum('bqkgh,bskh->bkgqs', query_blk, key_rot, preferred_element_type=jnp.float32) * score_scale
        query_idx = row_start + jnp.arange(block_len)
        allowed = key_idx[None, :] <= query_idx[:, None]
        scores = jnp.where(allowed, scores, -1e30)
        exp_scores = jnp.exp(scores - jnp.max(scores, axis=-1, keepdims=True))
        attn_probs = (exp_scores / jnp.sum(exp_scores, axis=-1, keepdims=True)).astype(jnp.bfloat16)
        context = jnp.einsum('bkgqs,bskh->bqkgh', attn_probs, value_seq, preferred_element_type=jnp.float32)
        return context.astype(jnp.bfloat16).reshape(batch_size, block_len, num_groups * group_cols)

    ctx_blocks = lax.map(one_block, jnp.arange(num_blocks))
    attn_part = jnp.einsum('nbqc,cd->bnqd', ctx_blocks, w_out_part, preferred_element_type=jnp.float32)
    return attn_part.reshape(batch_size, seq_len, model_width)


def solution(mesh):
    def local_layer(hidden_blk, attn_gain, attn_bias, mlp_gain, mlp_bias, w_qkv_part, w_out_part, w_up_part, w_down_part, positions):
        normed_attn = layer_norm(hidden_blk, attn_gain, attn_bias)
        normed_mlp = layer_norm(hidden_blk, mlp_gain, mlp_bias)
        attn_in = lax.all_gather(normed_attn, 'tp', axis=1, tiled=True)
        mlp_in = lax.all_gather(normed_mlp, 'tp', axis=1, tiled=True)
        attn_part = attention_branch(attn_in, w_qkv_part, w_out_part, positions)
        up_pre = jnp.einsum('bsd,df->bsf', mlp_in, w_up_part, preferred_element_type=jnp.float32)
        up_act = jax.nn.gelu(up_pre, approximate=False).astype(jnp.bfloat16)
        mlp_part = jnp.einsum('bsf,fd->bsd', up_act, w_down_part, preferred_element_type=jnp.float32)
        token_sum = lax.psum_scatter(attn_part + mlp_part, 'tp', scatter_dimension=1, tiled=True)
        return (hidden_blk.astype(jnp.float32) + token_sum).astype(jnp.bfloat16)

    return jax.shard_map(local_layer, mesh=mesh, in_specs=(P('dp', 'tp', None), P(), P(), P(), P(), P(None, 'tp', None), P('tp', None), P(None, 'tp'), P('tp', None), P()), out_specs=P('dp', 'tp', None), check_vma=False)
```

profile of v0, /device:TPU:0, one launch (start us, length us, event | category | flops | bytes accessed | tf_op | source)
XLA Modules:
  0.0 179.4 jit_solution(15250845981701852063)
XLA Ops:
  6.5 0.0 all-gather.3.cloned.1.call-start
  6.5 1.3 convert_reduce_fusion
  7.8 1.4 fusion.64
  9.3 2.6 %fusion.61 = (bf16[1,64,5120]{2,1,0:T(8,128)(2,1)}, bf16[1,64,5120]{2,1,0:T(8,128)(2,1)}) fusion(bf16[1,64,5120]{2,1,0:T(8,128)(2,1)} %param.10, f32[5120]{0:T(1024)} %param.12, f32[5120]{0:T(1024)} %param.11, f32[64]{0:T(128)S(1)} %add_rsqrt_fusion, f32[64]{0:T(128)S(1)} %broadcast_multiply_fusion.1, f32[5120]{0:T(1024)} %param.14, f32[5120]{0:T(1024)} %param.13), kind=kLoop, calls=%fused_computation.73 | loop fusion | flops 2949120 | bytes 2048512 | tf_op jit(solution)/shard_map/convert_element_type | solution.py:12
  11.9 0.0 all-gather.3.cloned.1.call-update
  11.9 0.0 all-gather.5.cloned.1.call-start
  11.9 0.7 all-gather.5.cloned.1.call-update
  12.7 0.0 reduce-scatter.2.cloned.1.call-start
  12.8 0.7 convert_element_type.77
  13.4 0.1 broadcast_multiply_fusion
  13.5 0.5 fusion.84
  14.0 23.3 %all-gather.3.cloned.1.call-done = bf16[1,256,5120]{2,1,0:T(8,128)(2,1)} async-done(((bf16[1,64,5120]{2,1,0:T(8,128)(2,1)}), bf16[1,256,5120]{2,1,0:T(8,128)(2,1)}) %all-gather.3.cloned.1.call-update) | async-done | bytes 2621456 | tf_op jit(solution)/shard_map/all_gather | solution.py:68
  37.3 19.5 %fusion.53 = bf16[256,10,384]{2,0,1:T(8,128)(2,1)} fusion(bf16[5120,10,384]{2,0,1:T(8,128)(2,1)} %param.15, bf16[1,256,5120]{2,1,0:T(8,128)(2,1)} %all-gather.3.cloned.1.call-done), kind=kOutput, calls=%fused_computation.64 | convolution fusion | flops 10067312640 | bytes 43909120 | tf_op jit(solution)/shard_map/bsd,dkc->bskc/dot_general | solution.py:36
  56.8 2.7 %copy.15 = bf16[256,10,384]{0,2,1:T(8,128)(2,1)S(1)} copy(bf16[256,10,384]{2,0,1:T(8,128)(2,1)} %fusion.53) | data formatting | bytes 3932160 | tf_op jit(solution)/shard_map/convert_element_type | solution.py:36
  59.5 0.3 convert_bitcast_fusion
  59.8 0.1 fusion.77
  59.9 0.1 slice_negate_fusion
  60.0 0.9 fusion.52
  60.9 0.6 fusion.51
  61.5 0.9 convolution_convert_fusion
  62.4 0.0 all-gather.5.cloned.1.call-done
  62.4 31.2 %fusion.132 = bf16[256,5120]{1,0:T(8,128)(2,1)} fusion(bf16[5120,5120]{1,0:T(8,128)(2,1)} %param.17, bf16[1,256,5120]{2,1,0:T(8,128)(2,1)} %all-gather.5.cloned.1.call-done), kind=kOutput, calls=%fused_computation.5.clone.clone.1 | convolution fusion | flops 13506969600 | bytes 57671680 | tf_op jit(solution)/shard_map/bsd,df->bsf/dot_general | solution.py:71
  93.6 21.6 %fusion.11 = f32[256,5120]{1,0:T(8,128)S(1)} fusion(bf16[5120,5120]{1,0:T(8,128)(2,1)} %param.18, bf16[256,5120]{1,0:T(8,128)(2,1)} %fusion.132), kind=kOutput, calls=%fused_computation.21 | convolution fusion | flops 13421772800 | bytes 60293120 | tf_op jit(solution)/shard_map/bsf,fd->bsd/dot_general | solution.py:73
  115.2 10.4 %fusion = f32[1,256,5120]{2,1,0:T(8,128)} fusion(f32[256,5120]{1,0:T(8,128)S(1)} %fusion.11, bf16[256,1280]{0,1:T(8,128)(2,1)S(1)} %bitcast.87, bf16[1280,5120]{1,0:T(8,128)(2,1)} %param.16), kind=kOutput, calls=%fused_computation.2 | convolution fusion | flops 3356753920 | bytes 24248320 | tf_op jit(solution)/shard_map/nbqc,cd->bnqd/dot_general | solution.py:60
  125.6 0.0 copy-start
  125.6 0.0 reduce-scatter.2.cloned.1.call-update
  125.7 45.0 %reduce-scatter.2.cloned.1.call-done = f32[1,64,5120]{2,1,0:T(8,128)} async-done(((f32[1,256,5120]{2,1,0:T(8,128)}), f32[1,64,5120]{2,1,0:T(8,128)}) %reduce-scatter.2.cloned.1.call-update) | async-done | bytes 1310736 | tf_op jit(solution)/shard_map/reduce_scatter | solution.py:74
  170.6 0.0 copy-done
  170.6 2.3 %fusion.68 = bf16[1,64,5120]{2,1,0:T(8,128)(2,1)} fusion(f32[1,64,5120]{2,1,0:T(8,128)} %reduce-scatter.2.cloned.1.call-done, bf16[1,64,5120]{2,1,0:T(8,128)(2,1)S(1)} %copy-done), kind=kLoop, calls=%fused_computation.80 | loop fusion | flops 983040 | bytes 2621440 | tf_op jit(solution)/shard_map/convert_element_type | solution.py:75
  (4 shorter events, 0.0 us)
Async XLA Ops:
  6.5 30.8 %all-gather.3.cloned.1.call-start = ((), (), s32[]{:S(2)}) async-start(), calls=%async_computation.1 | async-start | bytes 3276800 | tf_op jit(solution)/shard_map/all_gather | solution.py:68
  11.9 50.5 %all-gather.5.cloned.1.call-start = ((), (), s32[]{:S(2)}) async-start(), calls=%async_computation.2 | async-start | bytes 3276800 | tf_op jit(solution)/shard_map/all_gather | solution.py:69
  12.7 158.0 %reduce-scatter.2.cloned.1.call-start = ((), (), s32[]{:S(2)}) async-start(), calls=%async_computation.3 | async-start | bytes 6553600 | tf_op jit(solution)/shard_map/reduce_scatter | solution.py:74
  125.6 45.0 %copy-start = (bf16[1,64,5120]{2,1,0:T(8,128)(2,1)S(1)}, bf16[1,64,5120]{2,1,0:T(8,128)(2,1)}, u32[]{:S(2)}) copy-start(bf16[1,64,5120]{2,1,0:T(8,128)(2,1)} %param.10) | copy-start | bytes 1966084
Sparse Core Ops, SparseCore 0:
  12.0 25.2 all-gather.2
  38.8 22.4 all-gather.4
  125.8 44.7 reduce-scatter.1
where the time goes:
time: 180 us; the launch traced here: 179 us
  matrix products  84.5 us (47%)
  waiting for transfers between devices  69.1 us (38%)
  between operations  13.2 us (7%)
  other arithmetic  9.92 us (6%)
  local copies, waits for them, and re-layouts  2.68 us (1%)
    reduce_scatter x1, waiting for transfers between devices, local_layer(): lax.psum_scatter(attn_part + mlp_part, 'tp', scatter_dimension=1, tiled=T...  45 us
    dot_general x1, matrix products, local_layer(): jnp.einsum('bsd,df->bsf', mlp_in, w_up_part, preferred_element_type=jnp.f...  31.2 us
    all_gather x1, waiting for transfers between devices, local_layer(): attn_in = lax.all_gather(normed_attn, 'tp', axis=1, tiled=True)  23.3 us
    dot_general x1, matrix products, local_layer(): jnp.einsum('bsf,fd->bsd', up_act, w_down_part, preferred_element_type=jnp...  21.6 us
    dot_general x1, matrix products, attention_branch(): jnp.einsum('bsd,dkc->bskc', normed, w_qkv_part, preferred_element_type=jn...  19.5 us
    dot_general x1, matrix products, attention_branch(): jnp.einsum('nbqc,cd->bnqd', ctx_blocks, w_out_part, preferred_element_typ...  10.4 us
  transfers between devices with their start and end apart: 3, of which 2 were waited for; matrix products, arithmetic and copies ran while one was open for 15% of the time, Pallas kernels for 0%

commit v1 on v0

v1 whole, which is shorter than its diff:
```python
import jax
import jax.numpy as jnp
from jax import lax
from jax.experimental import pallas as pl
from jax.experimental.pallas import tpu as pltpu
from jax.sharding import PartitionSpec as P

MESH = pl.DeviceIdType.MESH
F32 = jnp.float32
BF16 = jnp.bfloat16

D = 5120
T = 256
TB = 64
HD = 128
G = 10
FF = 5120
NB = 512
CTX = G * HD
RING = 6
WORING = 3
N_UP = FF // NB
N_V = 3
N_QK = G // 2
N_DN = D // NB
V0 = N_UP
QK0 = V0 + N_V
DN0 = QK0 + N_QK
N_ITEMS = DN0 + N_DN
NPIECE = 4
PROWS = TB // NPIECE


def body(x_hbm, ga_hbm, ba_hbm, gm_hbm, bm_hbm, wqkv_hbm, wo_hbm, wup_hbm, wdn_hbm, pos_hbm,
         out_hbm,
         xall, a_all, m_all, act, ctx, v_all, acc, cos_t, sin_t, norms, pos_v,
         ring, woring, part, ra, sb, rb, outv,
         ring_sem, wo_sem, misc_sem, x_send, x_recv, c_send, c_recv, f_send, f_recv,
         a_send, a_recv, b_send, b_recv, out_sem):
    t = lax.axis_index("tp")
    partner = t + 1 - 2 * lax.rem(t, 2)
    cross = lax.rem(t + 2, 4)
    diag = lax.rem(partner + 2, 4)

    def local(src, dst, sem):
        return pltpu.make_async_copy(src, dst, sem)

    def remote(src, dst, ssem, rsem, dev):
        return pltpu.make_async_remote_copy(src_ref=src, dst_ref=dst, send_sem=ssem, recv_sem=rsem,
                                            device_id={"tp": dev}, device_id_type=MESH)

    def cols(i, n=NB):
        return pl.ds(pl.multiple_of(i * n, n), n)

    def issue_up(g):
        s = lax.rem(g, RING)
        local(wup_hbm.at[:, cols(g)], ring.at[s], ring_sem.at[s]).start()

    def issue_v(j, s):
        for h in range(4 if j < 2 else 2):
            local(wqkv_hbm.at[4 * j + h, :, pl.ds(2 * HD, HD)], ring.at[s, :, pl.ds(h * HD, HD)], ring_sem.at[s]).start()

    def issue_qk(g):
        s = lax.rem(g, RING)
        j = g - QK0
        for h in range(2):
            local(wqkv_hbm.at[2 * j + h, :, pl.ds(0, 2 * HD)], ring.at[s, :, pl.ds(h * 2 * HD, 2 * HD)], ring_sem.at[s]).start()

    def issue_dn(g):
        s = lax.rem(g, RING)
        j = g - DN0
        local(wdn_hbm.at[:, cols(j)], ring.at[s], ring_sem.at[s]).start()

    def issue_wo(j):
        w = lax.rem(j, WORING)
        local(wo_hbm.at[:, cols(j)], woring.at[w], wo_sem.at[w]).start()

    def issue(g):
        @pl.when(g < V0)
        def _():
            issue_up(g)
        for j in range(N_V):
            @pl.when(g == V0 + j)
            def _(j=j):
                issue_v(j, (V0 + j) % RING)

        @pl.when(jnp.logical_and(g >= QK0, g < DN0))
        def _():
            issue_qk(g)

        @pl.when(jnp.logical_and(g >= DN0, g < N_ITEMS))
        def _():
            issue_dn(g)

    def wait_ring(g):
        s = lax.rem(g, RING)
        local(wup_hbm.at[:, pl.ds(0, NB)], ring.at[s], ring_sem.at[s]).wait()
        return s

    xc = local(x_hbm, xall.at[t], misc_sem.at[0])
    xc.start()
    small = [local(h, norms.at[pl.ds(i, 1), :], misc_sem.at[1 + i]) for i, h in enumerate((ga_hbm, ba_hbm, gm_hbm, bm_hbm))]
    small.append(local(pos_hbm, pos_v, misc_sem.at[5]))
    for c in small:
        c.start()
    barrier = pltpu.get_barrier_semaphore()
    for dev in (partner, cross):
        pl.semaphore_signal(barrier, inc=1, device_id={"tp": dev}, device_id_type=MESH)
    for g in range(RING):
        issue_up(g)
    pl.semaphore_wait(barrier, 2)
    xc.wait()

    def piece(i):
        return pl.ds(i * PROWS, PROWS)

    to_cross = [remote(xall.at[t, piece(i)], xall.at[t, piece(i)], c_send.at[i], c_recv.at[i], cross) for i in range(NPIECE)]
    for c in to_cross:
        c.start()
    to_partner = remote(xall.at[t], xall.at[t], x_send.at[0], x_recv.at[0], partner)
    to_partner.start()
    from_cross = [remote(xall.at[cross, piece(i)], xall.at[cross, piece(i)], c_send.at[i], c_recv.at[i], cross) for i in range(NPIECE)]
    from_partner = remote(xall.at[partner], xall.at[partner], x_send.at[0], x_recv.at[0], partner)
    forward = [remote(xall.at[cross, piece(i)], xall.at[cross, piece(i)], f_send.at[i], f_recv.at[i], partner) for i in range(NPIECE)]
    from_fwd = [remote(xall.at[diag, piece(i)], xall.at[diag, piece(i)], f_send.at[i], f_recv.at[i], partner) for i in range(NPIECE)]

    for c in small:
        c.wait()

    lane = lax.broadcasted_iota(jnp.int32, (HD, T), 0)
    half = jnp.where(lane < HD // 2, lane, lane - HD // 2).astype(F32)
    inv_freq = jnp.exp(half * (-2.0 / HD) * 9.210340371976184)
    ang = pos_v[...].astype(F32) * inv_freq
    cos_t[...] = jnp.cos(ang).T
    sin_t[...] = jnp.where(lane < HD // 2, -jnp.sin(ang), jnp.sin(ang)).T
    acc[...] = jnp.zeros_like(acc)

    LR = 16

    def norm_rows(blk, row0):
        xr = xall[blk, pl.ds(row0, LR), :].astype(F32)
        mean = jnp.mean(xr, axis=-1, keepdims=True)
        cen = xr - mean
        var = jnp.mean(cen * cen, axis=-1, keepdims=True)
        z = cen * lax.rsqrt(var + 1e-5)
        dst = pl.ds(pl.multiple_of(blk * TB + row0, LR), LR)
        a_all[dst, :] = (z * norms[0:1, :] + norms[1:2, :]).astype(BF16)
        m_all[dst, :] = (z * norms[2:3, :] + norms[3:4, :]).astype(BF16)

    def norm_block(blk, start, n):
        def step(i, carry):
            norm_rows(blk, pl.multiple_of(start + i * LR, LR))
            return carry
        lax.fori_loop(0, n // LR, step, 0)

    norm_block(t, 0, TB)
    from_partner.wait_recv()
    norm_block(partner, 0, TB)
    for i in range(NPIECE):
        from_cross[i].wait_recv()
        forward[i].start()
        norm_block(cross, i * PROWS, PROWS)
        if i:
            from_fwd[i - 1].wait_recv()
            norm_block(diag, (i - 1) * PROWS, PROWS)
    from_fwd[NPIECE - 1].wait_recv()
    norm_block(diag, (NPIECE - 1) * PROWS, PROWS)

    def gelu_store(j):
        u = acc[...]
        act[:, cols(j)] = (0.5 * u * (1.0 + lax.erf(u * 0.7071067811865476))).astype(BF16)

    def up_step(g, carry):
        s = wait_ring(g)

        @pl.when(g >= 1)
        def _():
            issue(g + RING - 1)
        gelu_store(jnp.maximum(g - 1, 0))
        acc[...] = jnp.dot(m_all[...], ring[s], preferred_element_type=F32)
        return carry

    lax.fori_loop(0, N_UP, up_step, 0)

    for j in range(N_V):
        g = V0 + j
        s = g % RING
        n = NB if j < 2 else NB // 2
        local(wup_hbm.at[:, pl.ds(0, n)], ring.at[s, :, pl.ds(0, n)], ring_sem.at[s]).wait()
        issue(jnp.int32(g + RING - 1))
        if j == 0:
            gelu_store(N_UP - 1)
        v_all[:, pl.ds(j * NB, n)] = jnp.dot(a_all[...], ring[s, :, pl.ds(0, n)], preferred_element_type=F32).astype(BF16)

    def attend(j):
        def rot(u):
            u = u.astype(BF16).astype(F32)
            return (u * cos_t[...] + pltpu.roll(u, HD // 2, 1) * sin_t[...]).astype(BF16)

        mask = lax.broadcasted_iota(jnp.int32, (T, T), 1) <= lax.broadcasted_iota(jnp.int32, (T, T), 0)
        for h in range(2):
            q = rot(acc[:, pl.ds(2 * h * HD, HD)])
            k = rot(acc[:, pl.ds((2 * h + 1) * HD, HD)])
            hcol = pl.ds(pl.multiple_of((2 * j + h) * HD, HD), HD)
            v = v_all[:, hcol]
            sc = lax.dot_general(q, k, (((1,), (1,)), ((), ())), preferred_element_type=F32) * (HD ** -0.5)
            sc = jnp.where(mask, sc, -1e30)
            e = jnp.exp(sc - jnp.max(sc, axis=-1, keepdims=True))
            p = (e * (1.0 / jnp.sum(e, axis=-1, keepdims=True))).astype(BF16)
            ctx[:, hcol] = jnp.dot(p, v, preferred_element_type=F32).astype(BF16)

    acc[...] = jnp.zeros_like(acc)
    for j in range(WORING - 1):
        issue_wo(j)

    def qk_step(g, carry):
        s = wait_ring(g)
        issue(g + RING - 1)
        attend(jnp.maximum(g - QK0 - 1, 0))
        acc[...] = jnp.dot(a_all[...], ring[s], preferred_element_type=F32)
        return carry

    lax.fori_loop(QK0, DN0, qk_step, 0)
    attend(N_QK - 1)

    def rows(blk):
        return pl.ds(pl.multiple_of(blk * TB, TB), TB)

    def a_copy(j, i):
        blk = partner if i == 0 else diag
        return remote(part.at[j, rows(blk)], ra.at[j, i], a_send.at[j, i], a_recv.at[j, i], partner)

    def b_copy(j):
        return remote(sb.at[j], rb.at[j], b_send.at[j], b_recv.at[j], cross)

    def do_a(j):
        for i in range(2):
            a_copy(j, i).start()

    def do_b(j):
        for i in range(2):
            a_copy(j, i).wait_recv()
        sb[j] = (part[j, rows(cross), :] + ra[j, 1]).astype(BF16)
        b_copy(j).start()

    def out_copy(j):
        return local(outv.at[:, cols(j)], out_hbm.at[:, cols(j)], out_sem.at[j])

    def do_c(j):
        b_copy(j).wait_recv()
        tot = (part[j, rows(t), :] + ra[j, 0]) + rb[j].astype(F32)
        outv[:, cols(j)] = (xall[t, :, cols(j)].astype(F32) + tot).astype(BF16)
        out_copy(j).start()

    def dn_step(j, carry):
        g = j + DN0
        s = wait_ring(g)
        w = lax.rem(j, WORING)
        local(wo_hbm.at[:, pl.ds(0, NB)], woring.at[w], wo_sem.at[w]).wait()

        @pl.when(j >= 1)
        def _():
            do_a(j - 1)

        @pl.when(j + DN0 + RING - 1 < N_ITEMS)
        def _():
            issue(g + RING - 1)

        @pl.when(j + WORING - 1 < N_DN)
        def _():
            issue_wo(j + WORING - 1)

        @pl.when(j >= 2)
        def _():
            do_b(j - 2)

        @pl.when(j >= 4)
        def _():
            do_c(j - 4)
        part[j] = jnp.dot(act[...], ring[s], preferred_element_type=F32) + jnp.dot(ctx[...], woring[w], preferred_element_type=F32)
        return carry

    lax.fori_loop(0, N_DN, dn_step, 0)
    do_a(N_DN - 1)
    do_b(N_DN - 2)
    do_c(N_DN - 4)
    do_b(N_DN - 1)
    for j in range(N_DN - 3, N_DN):
        do_c(j)

    for c in to_cross + [to_partner] + forward:
        c.wait_send()

    def drain(j, carry):
        for i in range(2):
            a_copy(j, i).wait_send()
        b_copy(j).wait_send()
        out_copy(j).wait()
        return carry

    lax.fori_loop(0, N_DN, drain, 0)


def solution(mesh):
    def local_layer(hidden_blk, attn_gain, attn_bias, mlp_gain, mlp_bias, w_qkv, w_out, w_up, w_down, positions):
        args = (hidden_blk.reshape(TB, D), attn_gain.reshape(1, D), attn_bias.reshape(1, D), mlp_gain.reshape(1, D),
                mlp_bias.reshape(1, D), jnp.transpose(w_qkv, (1, 0, 2)), w_out, w_up, w_down, positions.reshape(1, T))
        dma = pltpu.SemaphoreType.DMA
        out = pl.pallas_call(
            body,
            out_shape=jax.ShapeDtypeStruct((TB, D), BF16),
            in_specs=[pl.BlockSpec(memory_space=pl.ANY)] * 10,
            out_specs=pl.BlockSpec(memory_space=pl.ANY),
            scratch_shapes=[
                pltpu.VMEM((4, TB, D), BF16),
                pltpu.VMEM((T, D), BF16),
                pltpu.VMEM((T, D), BF16),
                pltpu.VMEM((T, FF), BF16),
                pltpu.VMEM((T, CTX), BF16),
                pltpu.VMEM((T, CTX), BF16),
                pltpu.VMEM((T, NB), F32),
                pltpu.VMEM((T, HD), F32),
                pltpu.VMEM((T, HD), F32),
                pltpu.VMEM((4, D), F32),
                pltpu.VMEM((1, T), jnp.int32),
                pltpu.VMEM((RING, D, NB), BF16),
                pltpu.VMEM((WORING, CTX, NB), BF16),
                pltpu.VMEM((N_DN, T, NB), F32),
                pltpu.VMEM((N_DN, 2, TB, NB), F32),
                pltpu.VMEM((N_DN, TB, NB), BF16),
                pltpu.VMEM((N_DN, TB, NB), BF16),
                pltpu.VMEM((TB, D), BF16),
                dma((RING,)), dma((WORING,)), dma((6,)), dma((1,)), dma((1,)), dma((NPIECE,)), dma((NPIECE,)),
                dma((NPIECE,)), dma((NPIECE,)), dma((N_DN, 2)), dma((N_DN, 2)), dma((N_DN,)), dma((N_DN,)), dma((N_DN,)),
            ],
            compiler_params=pltpu.CompilerParams(collective_id=0, has_side_effects=True, vmem_limit_bytes=67043328),
            cost_estimate=pl.CostEstimate(flops=40_300_000_000, bytes_accessed=158_000_000, transcendentals=2_000_000),
            name="layer",
        )(*args)
        return out.reshape(1, TB, D)

    return jax.shard_map(local_layer, mesh=mesh,
                         in_specs=(P('dp', 'tp', None), P(), P(), P(), P(), P(None, 'tp', None), P('tp', None), P(None, 'tp'), P('tp', None), P()),
                         out_specs=P('dp', 'tp', None), check_vma=False)
```

time: 180 us -> 82.6 us (0.46)
  matrix products: 84.5 us -> 0 us
  Pallas kernels: 0 us -> 80.5 us
  waiting for transfers between devices: 69.1 us -> 0 us
  between operations: 13.2 us -> 0.01 us
  other arithmetic: 9.92 us -> 0 us
    dot_general x6 -> x0, matrix products: 84.5 us -> none  [the longest x1 31.2 us: local_layer(): jnp.einsum('bsd,df->bsf', mlp_in, w_up_part, preferred_element_type=jnp.f...]
    pallas_call x0 -> x1, Pallas kernels: none -> 80.5 us  [local_layer(): pl.pallas_call(body, out_shape=jax.ShapeDtypeStruct((TB, D), BF16), in_sp...]
    reduce_scatter x1 -> x0, waiting for transfers between devices: 45 us -> none  [local_layer(): lax.psum_scatter(attn_part + mlp_part, 'tp', scatter_dimension=1, tiled=T...]
    all_gather x2 -> x0, waiting for transfers between devices: 23.4 us -> none  [the longest x1 23.3 us: local_layer(): attn_in = lax.all_gather(normed_attn, 'tp', axis=1, tiled=True)]
    convert_element_type x4 -> x0, other arithmetic: 5.84 us -> none  [the longest x1 2.61 us: layer_norm(): (centered * lax.rsqrt(row_var + 1e-05) * norm_gain + norm_bias).astype(jn...]
    reduce_sum x3 -> x0, other arithmetic: 3.25 us -> none  [the longest x1 1.43 us: layer_norm(): row_var = jnp.mean(centered * centered, axis=-1, keepdims=True)]
    convert_element_type x1 -> x0, local copies, waits for them, and re-layouts: 2.67 us -> none  [attention_branch(): jnp.einsum('bsd,dkc->bskc', normed, w_qkv_part, preferred_element_type=jn...]
    unnamed x2 -> x1, local copies, waits for them, and re-layouts: 0.01 us -> 1.97 us
  transfers between devices with their start and end apart: 3 -> 0, of which waited for: 2 -> 0; matrix products, arithmetic and copies ran while one was open for 15% -> 0% of each run, Pallas kernels for 0% -> 0%
where the time goes in v1:
time: 82.6 us; the launch traced here: 82.5 us
  Pallas kernels  80.5 us (97%)
  local copies, waits for them, and re-layouts  1.97 us (2%)
    pallas_call x1, Pallas kernels, local_layer(): pl.pallas_call(body, out_shape=jax.ShapeDtypeStruct((TB, D), BF16), in_sp...  80.5 us
    unnamed x1, local copies, waits for them, and re-layouts  1.97 us

profile of v1, /device:TPU:0, one launch (start us, length us, event | category | flops | bytes accessed | tf_op | source)
XLA Modules:
  0.0 82.5 jit_solution(14313486826903013993)
XLA Ops:
  0.0 80.5 %layer.1 = bf16[64,5120]{1,0:T(8,128)(2,1)} custom-call(bf16[64,5120]{1,0:T(8,128)(2,1)} %bitcast.10, f32[1,5120]{1,0:T(1,128)} %bitcast.11, f32[1,5120]{1,0:T(1,128)} %bitcast.12, f32[1,5120]{1,0:T(1,128)} %bitcast.13, f32[1,5120]{1,0:T(1,128)} %bitcast.14, bf16[10,5120,384]{2,1,0:T(8,128)(2,1)} %bitcast.8, bf16[1280,5120]{1,0:T(8,128)(2,1)} %wo_hbm.1, ...), custom_call_target="tpu_custom_call" | custom-call | flops 40299999232 | bytes 158000000 | tf_op jit(solution)/shard_map/layer/pallas_call | solution.py:309
  80.5 2.0 %copy.12 = bf16[1,64,5120]{2,1,0:T(8,128)(2,1)} copy(bf16[1,64,5120]{2,1,0:T(8,128)(2,1)} %bitcast.9) | data formatting | bytes 1310720

commit v2 on v0

v2 whole, which is shorter than its diff:
```python
import jax
import jax.numpy as jnp
from jax import lax
from jax.experimental import pallas as pl
from jax.experimental.pallas import tpu as pltpu
from jax.sharding import PartitionSpec as P

MESH = pl.DeviceIdType.MESH
F32 = jnp.float32
BF16 = jnp.bfloat16

D = 5120
T = 256
TB = 64
HD = 128
G = 10
FF = 5120
NB = 512
CTX = G * HD
RING = 9
WORING = 2
N_QKV = 8
N_UP = FF // NB
N_DN = D // NB
UP0 = N_QKV
DN0 = UP0 + N_UP
N_ITEMS = DN0 + N_DN
NPIECE = 4
PROWS = TB // NPIECE
HALF = 2 * TB
RA = 4
KC = 2560


def body(x_hbm, ga_hbm, ba_hbm, gm_hbm, bm_hbm, wqkv_hbm, wo_hbm, wup_hbm, wdn_hbm, pos_hbm,
         out_hbm,
         x_own, abuf, ctx, acc, norms, pos_v,
         ring, woring, ra, sb, rb, out_v,
         ring_sem, wo_sem, misc_sem, x_send, x_recv, c_send, c_recv, f_send, f_recv,
         a_send, a_recv, b_send, b_recv, out_sem):
    t = lax.axis_index("tp")
    partner = t + 1 - 2 * lax.rem(t, 2)
    cross = lax.rem(t + 2, 4)
    diag = lax.rem(partner + 2, 4)
    near0 = pl.multiple_of((t // 2) * HALF, HALF)
    far0 = pl.multiple_of((1 - t // 2) * HALF, HALF)

    def local(src, dst, sem):
        return pltpu.make_async_copy(src, dst, sem)

    def remote(src, dst, ssem, rsem, dev):
        return pltpu.make_async_remote_copy(src_ref=src, dst_ref=dst, send_sem=ssem, recv_sem=rsem,
                                            device_id={"tp": dev}, device_id_type=MESH)

    def rows(blk, start=0, n=TB):
        return pl.ds(pl.multiple_of(blk * TB + start, 16), n)

    def cols(i, n=NB):
        return pl.ds(pl.multiple_of(i * n, n), n)

    def issue_qkv(p):
        if p in (0, 1, 7):
            j = {0: 0, 1: 1, 7: 2}[p]
            for h in range(4 if j < 2 else 2):
                local(wqkv_hbm.at[4 * j + h, :, pl.ds(2 * HD, HD)], ring.at[p, :, pl.ds(h * HD, HD)], ring_sem.at[p]).start()
        else:
            for h in range(2):
                local(wqkv_hbm.at[2 * (p - 2) + h, :, pl.ds(0, 2 * HD)], ring.at[p, :, pl.ds(h * 2 * HD, 2 * HD)], ring_sem.at[p]).start()

    def issue(g):
        s = lax.rem(g, RING)

        @pl.when(g < DN0)
        def _():
            local(wup_hbm.at[:, cols(g - UP0)], ring.at[s], ring_sem.at[s]).start()

        @pl.when(jnp.logical_and(g >= DN0, g < N_ITEMS))
        def _():
            local(wdn_hbm.at[:, cols(g - DN0)], ring.at[s], ring_sem.at[s]).start()

    def issue_wo(j):
        w = lax.rem(j, WORING)
        local(wo_hbm.at[:, cols(j)], woring.at[w], wo_sem.at[w]).start()

    def wait_ring(g, n=NB):
        s = lax.rem(g, RING)
        local(wup_hbm.at[:, pl.ds(0, n)], ring.at[s, :, pl.ds(0, n)], ring_sem.at[s]).wait()
        return s

    xc = local(x_hbm, x_own, misc_sem.at[0])
    xc.start()
    small = [local(h, norms.at[pl.ds(i, 1), :], misc_sem.at[1 + i]) for i, h in enumerate((ga_hbm, ba_hbm, gm_hbm, bm_hbm))]
    small.append(local(pos_hbm, pos_v, misc_sem.at[5]))
    for c in small:
        c.start()
    barrier = pltpu.get_barrier_semaphore()
    for dev in (partner, cross):
        pl.semaphore_signal(barrier, inc=1, device_id={"tp": dev}, device_id_type=MESH)
    for p in range(N_QKV):
        issue_qkv(p)
    issue(jnp.int32(UP0))
    xc.wait()
    pl.semaphore_wait(barrier, 2)

    to_cross = [remote(x_own.at[pl.ds(i * PROWS, PROWS)], abuf.at[rows(t, i * PROWS, PROWS)], c_send.at[i], c_recv.at[i], cross) for i in range(NPIECE)]
    for c in to_cross:
        c.start()
    to_partner = remote(x_own, abuf.at[rows(t)], x_send.at[0], x_recv.at[0], partner)
    to_partner.start()

    def cross_rows(i):
        return abuf.at[rows(cross, i * PROWS, PROWS)]

    def diag_rows(i):
        return abuf.at[rows(diag, i * PROWS, PROWS)]

    from_cross = [remote(cross_rows(i), cross_rows(i), c_send.at[i], c_recv.at[i], cross) for i in range(NPIECE)]
    from_partner = remote(abuf.at[rows(partner)], abuf.at[rows(partner)], x_send.at[0], x_recv.at[0], partner)
    forward = [remote(cross_rows(i), cross_rows(i), f_send.at[i], f_recv.at[i], partner) for i in range(NPIECE)]
    from_fwd = [remote(diag_rows(i), diag_rows(i), f_send.at[i], f_recv.at[i], partner) for i in range(NPIECE)]

    def gelu_store(j):
        u = acc[...]
        abuf[:, cols(j)] = (0.5 * u * (1.0 + lax.erf(u * 0.7071067811865476))).astype(BF16)

    def front(m_all, qkv, cos_t, sin_t):
        LR = 16

        def norm_rows(src, r_src, r_dst):
            xr = src[r_src, :].astype(F32)
            mean = jnp.mean(xr, axis=-1, keepdims=True)
            cen = xr - mean
            var = jnp.mean(cen * cen, axis=-1, keepdims=True)
            z = cen * lax.rsqrt(var + 1e-5)
            abuf[r_dst, :] = (z * norms[0:1, :] + norms[1:2, :]).astype(BF16)
            m_all[r_dst, :] = (z * norms[2:3, :] + norms[3:4, :]).astype(BF16)

        for c in small:
            c.wait()

        def own_step(i, carry):
            norm_rows(x_own, pl.ds(pl.multiple_of(i * LR, LR), LR), rows(t, i * LR, LR))
            return carry

        lax.fori_loop(0, TB // LR, own_step, 0)
        from_partner.wait_recv()

        def blk_step(i, carry):
            r = rows(partner, i * LR, LR)
            norm_rows(abuf, r, r)
            return carry

        lax.fori_loop(0, TB // LR, blk_step, 0)

        def norm_piece(blk, i):
            r = rows(blk, i * PROWS, PROWS)
            norm_rows(abuf, r, r)

        def qkv_half(p, r0):
            r = pl.ds(r0, HALF)
            qkv[p, r, :] = jnp.dot(abuf[r, :], ring[p], preferred_element_type=F32).astype(BF16)

        def qkv_last(r0):
            r = pl.ds(r0, HALF)
            p = N_QKV - 1
            n = NB // 2
            qkv[p, r, pl.ds(0, n)] = jnp.dot(abuf[r, :], ring[p, :, pl.ds(0, n)], preferred_element_type=F32).astype(BF16)

        def near_step(p, carry):
            wait_ring(p)

            @pl.when(p == 3)
            def _():
                from_cross[0].wait_recv()
                forward[0].start()

            @pl.when(p == 6)
            def _():
                from_cross[1].wait_recv()
                forward[1].start()
            qkv_half(p, near0)
            return carry

        lax.fori_loop(0, N_QKV - 1, near_step, 0)
        wait_ring(N_QKV - 1, NB // 2)
        qkv_last(near0)

        lane = lax.broadcasted_iota(jnp.int32, (HD, T), 0)
        half = jnp.where(lane < HD // 2, lane, lane - HD // 2).astype(F32)
        inv_freq = jnp.exp(half * (-2.0 / HD) * 9.210340371976184)
        ang = pos_v[...].astype(F32) * inv_freq
        cos_t[...] = jnp.cos(ang).T
        sin_t[...] = jnp.where(lane < HD // 2, -jnp.sin(ang), jnp.sin(ang)).T
        acc[...] = jnp.zeros_like(acc)

        forward[0].wait_send()
        norm_piece(cross, 0)
        from_fwd[0].wait_recv()
        norm_piece(diag, 0)
        for i in range(2, NPIECE):
            from_cross[i].wait_recv()
            forward[i].start()
            forward[i - 1].wait_send()
            norm_piece(cross, i - 1)
            from_fwd[i - 1].wait_recv()
            norm_piece(diag, i - 1)
        forward[NPIECE - 1].wait_send()
        norm_piece(cross, NPIECE - 1)
        from_fwd[NPIECE - 1].wait_recv()
        norm_piece(diag, NPIECE - 1)

        def far_step(p, carry):
            qkv_half(p, far0)
            issue(p + RING)
            return carry

        lax.fori_loop(0, N_QKV - 1, far_step, 0)
        qkv_last(far0)
        issue(jnp.int32(N_QKV - 1 + RING))
        for j in range(WORING):
            issue_wo(j)

        def rot(u):
            u = u.astype(F32)
            return (u * cos_t[...] + pltpu.roll(u, HD // 2, 1) * sin_t[...]).astype(BF16)

        def up_step(h, carry):
            g = h + UP0
            s = wait_ring(g)

            @pl.when(h >= 1)
            def _():
                issue(g - 1 + RING)
            qp = 2 + h // 2
            qc = pl.multiple_of(lax.rem(h, 2) * 2 * HD, 2 * HD)
            vp = jnp.where(h < 8, h // 4, N_QKV - 1)
            q = rot(qkv[qp, :, pl.ds(qc, HD)])
            k = rot(qkv[qp, :, pl.ds(qc + HD, HD)])
            first = jnp.dot(m_all[:, pl.ds(0, KC)], ring[s, pl.ds(0, KC), :], preferred_element_type=F32)
            sc = lax.dot_general(q, k, (((1,), (1,)), ((), ())), preferred_element_type=F32) * (HD ** -0.5)
            second = jnp.dot(m_all[:, pl.ds(KC, D - KC)], ring[s, pl.ds(KC, D - KC), :], preferred_element_type=F32)
            mask = lax.broadcasted_iota(jnp.int32, (T, T), 1) <= lax.broadcasted_iota(jnp.int32, (T, T), 0)
            sc = jnp.where(mask, sc, -1e30)
            e = jnp.exp(sc - jnp.max(sc, axis=-1, keepdims=True))
            pr = (e * (1.0 / jnp.sum(e, axis=-1, keepdims=True))).astype(BF16)
            v = qkv[vp, :, pl.ds(pl.multiple_of(lax.rem(h, 4) * HD, HD), HD)]
            ctx[:, cols(h, HD)] = jnp.dot(pr, v, preferred_element_type=F32).astype(BF16)
            gelu_store(jnp.maximum(h - 1, 0))
            acc[...] = first + second
            return carry

        lax.fori_loop(0, N_UP, up_step, 0)

    def back(part):
        def a_copy(j, i):
            blk = partner if i == 0 else diag
            return remote(part.at[j, rows(blk)], ra.at[lax.rem(j, RA), i], a_send.at[j, i], a_recv.at[j, i], partner)

        def b_copy(j):
            return remote(sb.at[j], rb.at[j], b_send.at[j], b_recv.at[j], cross)

        def do_a(j):
            for i in range(2):
                a_copy(j, i).start()

        def do_b(j):
            for i in range(2):
                a_copy(j, i).wait_recv()
            r = lax.rem(j, RA)
            sb[j] = (part[j, rows(cross), :] + ra[r, 1]).astype(BF16)
            b_copy(j).start()
            part[j, rows(t), :] = part[j, rows(t), :] + ra[r, 0]

        def out_copy(j):
            return local(out_v.at[:, cols(j)], out_hbm.at[:, cols(j)], out_sem.at[j])

        def do_c(j):
            b_copy(j).wait_recv()
            out_v[:, cols(j)] = (x_own[:, cols(j)].astype(F32) + (part[j, rows(t), :] + rb[j].astype(F32))).astype(BF16)
            out_copy(j).start()

        def wait_dn(j):
            s = wait_ring(j + DN0)
            w = lax.rem(j, WORING)
            local(wo_hbm.at[:, pl.ds(0, NB)], woring.at[w], wo_sem.at[w]).wait()
            return s, w

        KL = D - NB

        def out_dot(j, s, w):
            return (jnp.dot(abuf[:, pl.ds(0, KL)], ring[s, pl.ds(0, KL), :], preferred_element_type=F32)
                    + jnp.dot(ctx[...], woring[w], preferred_element_type=F32)
                    + jnp.dot(abuf[:, pl.ds(KL, NB)], ring[s, pl.ds(KL, NB), :], preferred_element_type=F32))

        s, w = wait_dn(jnp.int32(0))
        issue(jnp.int32(DN0 - 1 + RING))
        gelu_store(N_UP - 1)
        part[0] = out_dot(0, s, w)

        def dn_step(j, carry):
            g = j + DN0
            s, w = wait_dn(j)
            do_a(j - 1)
            issue(g + RING - 1)

            @pl.when(j + WORING - 1 < N_DN)
            def _():
                issue_wo(j + WORING - 1)

            @pl.when(j >= 2)
            def _():
                do_b(j - 2)

            @pl.when(j >= 4)
            def _():
                do_c(j - 4)
            part[j] = out_dot(j, s, w)
            return carry

        lax.fori_loop(1, N_DN, dn_step, 0)
        do_a(N_DN - 1)
        do_b(N_DN - 2)
        do_c(N_DN - 4)
        do_b(N_DN - 1)
        for j in range(N_DN - 3, N_DN):
            do_c(j)

        def drain(j, carry):
            for i in range(2):
                a_copy(j, i).wait_send()
            b_copy(j).wait_send()
            out_copy(j).wait()
            return carry

        lax.fori_loop(0, N_DN, drain, 0)

    pl.run_scoped(front, pltpu.VMEM((T, D), BF16), pltpu.VMEM((N_QKV, T, NB), BF16),
                  pltpu.VMEM((T, HD), F32), pltpu.VMEM((T, HD), F32))
    pl.run_scoped(back, pltpu.VMEM((N_DN, T, NB), F32))
    for c in to_cross + [to_partner]:
        c.wait_send()


def solution(mesh):
    def local_layer(hidden_blk, attn_gain, attn_bias, mlp_gain, mlp_bias, w_qkv, w_out, w_up, w_down, positions):
        args = (hidden_blk.reshape(TB, D), attn_gain.reshape(1, D), attn_bias.reshape(1, D), mlp_gain.reshape(1, D),
                mlp_bias.reshape(1, D), jnp.transpose(w_qkv, (1, 0, 2)), w_out, w_up, w_down, positions.reshape(1, T))
        dma = pltpu.SemaphoreType.DMA
        out = pl.pallas_call(
            body,
            out_shape=jax.ShapeDtypeStruct((TB, D), BF16),
            in_specs=[pl.BlockSpec(memory_space=pl.ANY)] * 10,
            out_specs=pl.BlockSpec(memory_space=pl.ANY),
            scratch_shapes=[
                pltpu.VMEM((TB, D), BF16),
                pltpu.VMEM((T, D), BF16),
                pltpu.VMEM((T, CTX), BF16),
                pltpu.VMEM((T, NB), F32),
                pltpu.VMEM((4, D), F32),
                pltpu.VMEM((1, T), jnp.int32),
                pltpu.VMEM((RING, D, NB), BF16),
                pltpu.VMEM((WORING, CTX, NB), BF16),
                pltpu.VMEM((RA, 2, TB, NB), F32),
                pltpu.VMEM((N_DN, TB, NB), BF16),
                pltpu.VMEM((N_DN, TB, NB), BF16),
                pltpu.VMEM((TB, D), BF16),
                dma((RING,)), dma((WORING,)), dma((6,)), dma((1,)), dma((1,)), dma((NPIECE,)), dma((NPIECE,)),
                dma((NPIECE,)), dma((NPIECE,)), dma((N_DN, 2)), dma((N_DN, 2)), dma((N_DN,)), dma((N_DN,)), dma((N_DN,)),
            ],
            compiler_params=pltpu.CompilerParams(collective_id=0, has_side_effects=True, vmem_limit_bytes=67043328),
            cost_estimate=pl.CostEstimate(flops=40_300_000_000, bytes_accessed=158_000_000, transcendentals=2_000_000),
            name="layer",
        )(*args)
        return out.reshape(1, TB, D)

    return jax.shard_map(local_layer, mesh=mesh,
                         in_specs=(P('dp', 'tp', None), P(), P(), P(), P(), P(None, 'tp', None), P('tp', None), P(None, 'tp'), P('tp', None), P()),
                         out_specs=P('dp', 'tp', None), check_vma=False)
```

time: 180 us -> 76.5 us (0.42)
  matrix products: 84.5 us -> 0 us
  Pallas kernels: 0 us -> 74.4 us
  waiting for transfers between devices: 69.1 us -> 0 us
  between operations: 13.2 us -> 0.01 us
  other arithmetic: 9.92 us -> 0 us
    dot_general x6 -> x0, matrix products: 84.5 us -> none  [the longest x1 31.2 us: local_layer(): jnp.einsum('bsd,df->bsf', mlp_in, w_up_part, preferred_element_type=jnp.f...]
    pallas_call x0 -> x1, Pallas kernels: none -> 74.4 us  [local_layer(): pl.pallas_call(body, out_shape=jax.ShapeDtypeStruct((TB, D), BF16), in_sp...]
    reduce_scatter x1 -> x0, waiting for transfers between devices: 45 us -> none  [local_layer(): lax.psum_scatter(attn_part + mlp_part, 'tp', scatter_dimension=1, tiled=T...]
    all_gather x2 -> x0, waiting for transfers between devices: 23.4 us -> none  [the longest x1 23.3 us: local_layer(): attn_in = lax.all_gather(normed_attn, 'tp', axis=1, tiled=True)]
    convert_element_type x4 -> x0, other arithmetic: 5.84 us -> none  [the longest x1 2.61 us: layer_norm(): (centered * lax.rsqrt(row_var + 1e-05) * norm_gain + norm_bias).astype(jn...]
    reduce_sum x3 -> x0, other arithmetic: 3.25 us -> none  [the longest x1 1.43 us: layer_norm(): row_var = jnp.mean(centered * centered, axis=-1, keepdims=True)]
    convert_element_type x1 -> x0, local copies, waits for them, and re-layouts: 2.67 us -> none  [attention_branch(): jnp.einsum('bsd,dkc->bskc', normed, w_qkv_part, preferred_element_type=jn...]
    unnamed x2 -> x1, local copies, waits for them, and re-layouts: 0.01 us -> 1.97 us
  transfers between devices with their start and end apart: 3 -> 0, of which waited for: 2 -> 0; matrix products, arithmetic and copies ran while one was open for 15% -> 0% of each run, Pallas kernels for 0% -> 0%
where the time goes in v2:
time: 76.5 us; the launch traced here: 76.4 us
  Pallas kernels  74.4 us (97%)
  local copies, waits for them, and re-layouts  1.97 us (3%)
    pallas_call x1, Pallas kernels, local_layer(): pl.pallas_call(body, out_shape=jax.ShapeDtypeStruct((TB, D), BF16), in_sp...  74.4 us
    unnamed x1, local copies, waits for them, and re-layouts  1.97 us

profile of v2, /device:TPU:0, one launch (start us, length us, event | category | flops | bytes accessed | tf_op | source)
XLA Modules:
  0.0 76.4 jit_solution(15586413909437859889)
XLA Ops:
  0.0 74.4 %layer.1 = bf16[64,5120]{1,0:T(8,128)(2,1)} custom-call(bf16[64,5120]{1,0:T(8,128)(2,1)} %bitcast.10, f32[1,5120]{1,0:T(1,128)} %bitcast.11, f32[1,5120]{1,0:T(1,128)} %bitcast.12, f32[1,5120]{1,0:T(1,128)} %bitcast.13, f32[1,5120]{1,0:T(1,128)} %bitcast.14, bf16[10,5120,384]{2,1,0:T(8,128)(2,1)} %bitcast.8, bf16[1280,5120]{1,0:T(8,128)(2,1)} %wo_hbm.1, ...), custom_call_target="tpu_custom_call" | custom-call | flops 40299999232 | bytes 158000000 | tf_op jit(solution)/shard_map/layer/pallas_call | solution.py:349
  74.4 2.0 %copy.12 = bf16[1,64,5120]{2,1,0:T(8,128)(2,1)} copy(bf16[1,64,5120]{2,1,0:T(8,128)(2,1)} %bitcast.9) | data formatting | bytes 1310720

commit v3 on v2

--- a/solution.py
+++ b/solution.py
@@ -18,7 +18,8 @@
 NB = 512
 CTX = G * HD
 RING = 9
-WORING = 2
+WORING = 3
+SB = 4
 N_QKV = 8
 N_UP = FF // NB
 N_DN = D // NB
@@ -28,14 +29,14 @@
 NPIECE = 4
 PROWS = TB // NPIECE
 HALF = 2 * TB
-RA = 4
+RA = 5
 KC = 2560
 
 
 def body(x_hbm, ga_hbm, ba_hbm, gm_hbm, bm_hbm, wqkv_hbm, wo_hbm, wup_hbm, wdn_hbm, pos_hbm,
          out_hbm,
-         x_own, abuf, ctx, acc, norms, pos_v,
-         ring, woring, ra, sb, rb, out_v,
+         x_own, abuf, ctx, norms, pos_v,
+         ring, woring, ra, sb, rb,
          ring_sem, wo_sem, misc_sem, x_send, x_recv, c_send, c_recv, f_send, f_recv,
          a_send, a_recv, b_send, b_recv, out_sem):
     t = lax.axis_index("tp")
@@ -78,9 +79,9 @@
         def _():
             local(wdn_hbm.at[:, cols(g - DN0)], ring.at[s], ring_sem.at[s]).start()
 
-    def issue_wo(j):
+    def issue_wo(j, c=None):
         w = lax.rem(j, WORING)
-        local(wo_hbm.at[:, cols(j)], woring.at[w], wo_sem.at[w]).start()
+        local(wo_hbm.at[:, cols(j if c is None else c)], woring.at[w], wo_sem.at[w]).start()
 
     def wait_ring(g, n=NB):
         s = lax.rem(g, RING)
@@ -119,11 +120,10 @@
     forward = [remote(cross_rows(i), cross_rows(i), f_send.at[i], f_recv.at[i], partner) for i in range(NPIECE)]
     from_fwd = [remote(diag_rows(i), diag_rows(i), f_send.at[i], f_recv.at[i], partner) for i in range(NPIECE)]
 
-    def gelu_store(j):
-        u = acc[...]
+    def gelu_store(u, j):
         abuf[:, cols(j)] = (0.5 * u * (1.0 + lax.erf(u * 0.7071067811865476))).astype(BF16)
 
-    def front(m_all, qkv, cos_t, sin_t):
+    def front(m_all, qkv, cos_t, sin_t, acc):
         LR = 16
 
         def norm_rows(src, r_src, r_dst):
@@ -209,14 +209,18 @@
         from_fwd[NPIECE - 1].wait_recv()
         norm_piece(diag, NPIECE - 1)
 
-        def far_step(p, carry):
-            qkv_half(p, far0)
-            issue(p + RING)
-            return carry
-
-        lax.fori_loop(0, N_QKV - 1, far_step, 0)
+        def far_step(i, carry):
+            for p in (2 * i, 2 * i + 1):
+                qkv_half(p, far0)
+            for p in (2 * i, 2 * i + 1):
+                issue(p + RING)
+            return carry
+
+        lax.fori_loop(0, N_QKV // 2 - 1, far_step, 0)
+        qkv_half(N_QKV - 2, far0)
         qkv_last(far0)
-        issue(jnp.int32(N_QKV - 1 + RING))
+        for p in (N_QKV - 2, N_QKV - 1):
+            issue(jnp.int32(p + RING))
         for j in range(WORING):
             issue_wo(j)
 
@@ -224,32 +228,45 @@
             u = u.astype(F32)
             return (u * cos_t[...] + pltpu.roll(u, HD // 2, 1) * sin_t[...]).astype(BF16)
 
-        def up_step(h, carry):
-            g = h + UP0
-            s = wait_ring(g)
-
-            @pl.when(h >= 1)
-            def _():
-                issue(g - 1 + RING)
+        def head(h, dot_a, dot_b):
             qp = 2 + h // 2
             qc = pl.multiple_of(lax.rem(h, 2) * 2 * HD, 2 * HD)
             vp = jnp.where(h < 8, h // 4, N_QKV - 1)
             q = rot(qkv[qp, :, pl.ds(qc, HD)])
             k = rot(qkv[qp, :, pl.ds(qc + HD, HD)])
-            first = jnp.dot(m_all[:, pl.ds(0, KC)], ring[s, pl.ds(0, KC), :], preferred_element_type=F32)
+            first = dot_a()
             sc = lax.dot_general(q, k, (((1,), (1,)), ((), ())), preferred_element_type=F32) * (HD ** -0.5)
-            second = jnp.dot(m_all[:, pl.ds(KC, D - KC)], ring[s, pl.ds(KC, D - KC), :], preferred_element_type=F32)
+            second = dot_b()
             mask = lax.broadcasted_iota(jnp.int32, (T, T), 1) <= lax.broadcasted_iota(jnp.int32, (T, T), 0)
             sc = jnp.where(mask, sc, -1e30)
             e = jnp.exp(sc - jnp.max(sc, axis=-1, keepdims=True))
             pr = (e * (1.0 / jnp.sum(e, axis=-1, keepdims=True))).astype(BF16)
             v = qkv[vp, :, pl.ds(pl.multiple_of(lax.rem(h, 4) * HD, HD), HD)]
             ctx[:, cols(h, HD)] = jnp.dot(pr, v, preferred_element_type=F32).astype(BF16)
-            gelu_store(jnp.maximum(h - 1, 0))
-            acc[...] = first + second
-            return carry
-
-        lax.fori_loop(0, N_UP, up_step, 0)
+            return first + second
+
+        def up_step(i, carry):
+            h0 = 2 * i
+            g0 = h0 + UP0
+            ss = [wait_ring(g0), wait_ring(g0 + 1)]
+
+            @pl.when(i >= 1)
+            def _():
+                issue(g0 - 2 + RING)
+                issue(g0 - 1 + RING)
+
+            def part_dot(s, lo):
+                r = pl.ds(lo, KC)
+                return lambda: jnp.dot(m_all[:, r], ring[s, r, :], preferred_element_type=F32)
+            gelu_store(acc[...], jnp.maximum(h0 - 1, 0))
+            u0 = head(h0, part_dot(ss[0], 0), part_dot(ss[0], KC))
+            gelu_store(u0, h0)
+            u1 = head(h0 + 1, part_dot(ss[1], 0), part_dot(ss[1], KC))
+            acc[...] = u1
+            return carry
+
+        lax.fori_loop(0, N_UP // 2, up_step, 0)
+        gelu_store(acc[...], N_UP - 1)
 
     def back(part):
         def a_copy(j, i):
@@ -257,7 +274,7 @@
             return remote(part.at[j, rows(blk)], ra.at[lax.rem(j, RA), i], a_send.at[j, i], a_recv.at[j, i], partner)
 
         def b_copy(j):
-            return remote(sb.at[j], rb.at[j], b_send.at[j], b_recv.at[j], cross)
+            return remote(sb.at[lax.rem(j, SB)], rb.at[j], b_send.at[j], b_recv.at[j], cross)
 
         def do_a(j):
             for i in range(2):
@@ -267,16 +284,20 @@
             for i in range(2):
                 a_copy(j, i).wait_recv()
             r = lax.rem(j, RA)
-            sb[j] = (part[j, rows(cross), :] + ra[r, 1]).astype(BF16)
+
+            @pl.when(j >= SB)
+            def _():
+                b_copy(j - SB).wait_send()
+            sb[lax.rem(j, SB)] = (part[j, rows(cross), :] + ra[r, 1]).astype(BF16)
             b_copy(j).start()
             part[j, rows(t), :] = part[j, rows(t), :] + ra[r, 0]
 
         def out_copy(j):
-            return local(out_v.at[:, cols(j)], out_hbm.at[:, cols(j)], out_sem.at[j])
+            return local(x_own.at[:, cols(j)], out_hbm.at[:, cols(j)], out_sem.at[j])
 
         def do_c(j):
             b_copy(j).wait_recv()
-            out_v[:, cols(j)] = (x_own[:, cols(j)].astype(F32) + (part[j, rows(t), :] + rb[j].astype(F32))).astype(BF16)
+            x_own[:, cols(j)] = (x_own[:, cols(j)].astype(F32) + (part[j, rows(t), :] + rb[j].astype(F32))).astype(BF16)
             out_copy(j).start()
 
         def wait_dn(j):
@@ -285,60 +306,74 @@
             local(wo_hbm.at[:, pl.ds(0, NB)], woring.at[w], wo_sem.at[w]).wait()
             return s, w
 
-        KL = D - NB
-
-        def out_dot(j, s, w):
-            return (jnp.dot(abuf[:, pl.ds(0, KL)], ring[s, pl.ds(0, KL), :], preferred_element_type=F32)
-                    + jnp.dot(ctx[...], woring[w], preferred_element_type=F32)
-                    + jnp.dot(abuf[:, pl.ds(KL, NB)], ring[s, pl.ds(KL, NB), :], preferred_element_type=F32))
-
-        s, w = wait_dn(jnp.int32(0))
-        issue(jnp.int32(DN0 - 1 + RING))
-        gelu_store(N_UP - 1)
-        part[0] = out_dot(0, s, w)
-
-        def dn_step(j, carry):
-            g = j + DN0
-            s, w = wait_dn(j)
-            do_a(j - 1)
-            issue(g + RING - 1)
-
-            @pl.when(j + WORING - 1 < N_DN)
-            def _():
-                issue_wo(j + WORING - 1)
-
-            @pl.when(j >= 2)
-            def _():
+        def out_dot(s, w):
+            return (jnp.dot(ctx[...], woring[w], preferred_element_type=F32)
+                    + jnp.dot(abuf[...], ring[s], preferred_element_type=F32))
+
+        def refill(j):
+            @pl.when(j + DN0 + RING < N_ITEMS)
+            def _():
+                issue(j + DN0 + RING)
+
+        for g in (DN0 - 2, DN0 - 1):
+            issue(jnp.int32(g + RING))
+
+        def dn_pair(i, carry):
+            j = 2 * i
+            s0, w0 = wait_dn(j)
+            s1, w1 = wait_dn(j + 1)
+
+            @pl.when(i >= 1)
+            def _():
+                do_a(j - 1)
+                refill(j - 2)
+                refill(j - 1)
+                issue_wo(j + 2, jnp.minimum(j + 2, N_DN - 1))
                 do_b(j - 2)
 
-            @pl.when(j >= 4)
-            def _():
-                do_c(j - 4)
-            part[j] = out_dot(j, s, w)
-            return carry
-
-        lax.fori_loop(1, N_DN, dn_step, 0)
+            @pl.when(i >= 2)
+            def _():
+                do_b(j - 3)
+
+            @pl.when(i >= 3)
+            def _():
+                do_c(j - 6)
+                do_c(j - 5)
+            part[j] = out_dot(s0, w0)
+            issue_wo(j + 3, jnp.minimum(j + 3, N_DN - 1))
+            part[j + 1] = out_dot(s1, w1)
+            do_a(j)
+            return carry
+
+        N_PAIR = 5
+        lax.fori_loop(0, N_PAIR, dn_pair, 0)
         do_a(N_DN - 1)
+        do_b(N_DN - 3)
         do_b(N_DN - 2)
-        do_c(N_DN - 4)
+        do_c(4)
+        do_c(5)
         do_b(N_DN - 1)
-        for j in range(N_DN - 3, N_DN):
+        for j in range(6, N_DN):
             do_c(j)
+
+        for j in (N_DN, N_DN + 1):
+            local(wo_hbm.at[:, pl.ds(0, NB)], woring.at[j % WORING], wo_sem.at[j % WORING]).wait()
+        for j in range(N_DN - SB, N_DN):
+            b_copy(j).wait_send()
 
         def drain(j, carry):
             for i in range(2):
                 a_copy(j, i).wait_send()
-            b_copy(j).wait_send()
             out_copy(j).wait()
             return carry
 
         lax.fori_loop(0, N_DN, drain, 0)
 
     pl.run_scoped(front, pltpu.VMEM((T, D), BF16), pltpu.VMEM((N_QKV, T, NB), BF16),
-                  pltpu.VMEM((T, HD), F32), pltpu.VMEM((T, HD), F32))
-    pl.run_scoped(back, pltpu.VMEM((N_DN, T, NB), F32))
+                  pltpu.VMEM((T, HD), F32), pltpu.VMEM((T, HD), F32), pltpu.VMEM((T, NB), F32))
     for c in to_cross + [to_partner]:
         c.wait_send()
+    pl.run_scoped(back, pltpu.VMEM((N_DN, T, NB), F32))
 
 
 def solution(mesh):
@@ -355,15 +390,13 @@
                 pltpu.VMEM((TB, D), BF16),
                 pltpu.VMEM((T, D), BF16),
                 pltpu.VMEM((T, CTX), BF16),
-                pltpu.VMEM((T, NB), F32),
                 pltpu.VMEM((4, D), F32),
                 pltpu.VMEM((1, T), jnp.int32),
                 pltpu.VMEM((RING, D, NB), BF16),
                 pltpu.VMEM((WORING, CTX, NB), BF16),
                 pltpu.VMEM((RA, 2, TB, NB), F32),
+                pltpu.VMEM((SB, TB, NB), BF16),
                 pltpu.VMEM((N_DN, TB, NB), BF16),
-                pltpu.VMEM((N_DN, TB, NB), BF16),
-                pltpu.VMEM((TB, D), BF16),
                 dma((RING,)), dma((WORING,)), dma((6,)), dma((1,)), dma((1,)), dma((NPIECE,)), dma((NPIECE,)),
                 dma((NPIECE,)), dma((NPIECE,)), dma((N_DN, 2)), dma((N_DN, 2)), dma((N_DN,)), dma((N_DN,)), dma((N_DN,)),
             ],

time: 76.5 us -> 80.8 us (1.056)
  Pallas kernels: 74.4 us -> 78.7 us
    pallas_call x1, Pallas kernels: 74.4 us -> 78.7 us  [local_layer(): pl.pallas_call(body, out_shape=jax.ShapeDtypeStruct((TB, D), BF16), in_sp...]
where the time goes in v3:
time: 80.8 us; the launch traced here: 80.7 us
  Pallas kernels  78.7 us (97%)
  local copies, waits for them, and re-layouts  1.97 us (2%)
    pallas_call x1, Pallas kernels, local_layer(): pl.pallas_call(body, out_shape=jax.ShapeDtypeStruct((TB, D), BF16), in_sp...  78.7 us
    unnamed x1, local copies, waits for them, and re-layouts  1.97 us

profile of v3, /device:TPU:0, one launch (start us, length us, event | category | flops | bytes accessed | tf_op | source)
XLA Modules:
  0.0 80.7 jit_solution(16697000487733059425)
XLA Ops:
  0.0 78.7 %layer.1 = bf16[64,5120]{1,0:T(8,128)(2,1)} custom-call(bf16[64,5120]{1,0:T(8,128)(2,1)} %bitcast.10, f32[1,5120]{1,0:T(1,128)} %bitcast.11, f32[1,5120]{1,0:T(1,128)} %bitcast.12, f32[1,5120]{1,0:T(1,128)} %bitcast.13, f32[1,5120]{1,0:T(1,128)} %bitcast.14, bf16[10,5120,384]{2,1,0:T(8,128)(2,1)} %bitcast.8, bf16[1280,5120]{1,0:T(8,128)(2,1)} %wo_hbm.1, ...), custom_call_target="tpu_custom_call" | custom-call | flops 40299999232 | bytes 158000000 | tf_op jit(solution)/shard_map/layer/pallas_call | solution.py:384
  78.7 2.0 %copy.12 = bf16[1,64,5120]{2,1,0:T(8,128)(2,1)} copy(bf16[1,64,5120]{2,1,0:T(8,128)(2,1)} %bitcast.9) | data formatting | bytes 1310720

commit v4 on v3

--- a/solution.py
+++ b/solution.py
@@ -79,9 +79,9 @@
         def _():
             local(wdn_hbm.at[:, cols(g - DN0)], ring.at[s], ring_sem.at[s]).start()
 
-    def issue_wo(j, c=None):
+    def issue_wo(j):
         w = lax.rem(j, WORING)
-        local(wo_hbm.at[:, cols(j if c is None else c)], woring.at[w], wo_sem.at[w]).start()
+        local(wo_hbm.at[:, cols(j)], woring.at[w], wo_sem.at[w]).start()
 
     def wait_ring(g, n=NB):
         s = lax.rem(g, RING)
@@ -328,36 +328,55 @@
                 do_a(j - 1)
                 refill(j - 2)
                 refill(j - 1)
-                issue_wo(j + 2, jnp.minimum(j + 2, N_DN - 1))
+                issue_wo(j + 2)
+
+            @pl.when(i >= 2)
+            def _():
+                do_b(j - 3)
+
+            @pl.when(i >= 1)
+            def _():
                 do_b(j - 2)
 
-            @pl.when(i >= 2)
-            def _():
-                do_b(j - 3)
+            @pl.when(i >= 4)
+            def _():
+                do_c(j - 7)
 
             @pl.when(i >= 3)
             def _():
                 do_c(j - 6)
-                do_c(j - 5)
             part[j] = out_dot(s0, w0)
-            issue_wo(j + 3, jnp.minimum(j + 3, N_DN - 1))
-            part[j + 1] = out_dot(s1, w1)
+            lo, hi = pl.ds(0, KC), pl.ds(KC, FF - KC)
+            first = (jnp.dot(ctx[...], woring[w1], preferred_element_type=F32)
+                     + jnp.dot(abuf[:, lo], ring[s1, lo, :], preferred_element_type=F32))
+            issue_wo(j + 3)
             do_a(j)
-            return carry
-
-        N_PAIR = 5
-        lax.fori_loop(0, N_PAIR, dn_pair, 0)
-        do_a(N_DN - 1)
-        do_b(N_DN - 3)
-        do_b(N_DN - 2)
+            part[j + 1] = first + jnp.dot(abuf[:, hi], ring[s1, hi, :], preferred_element_type=F32)
+            return carry
+
+        lax.fori_loop(0, N_DN // 2 - 1, dn_pair, 0)
+        s, w = wait_dn(N_DN - 2)
+        do_a(7)
+        do_b(5)
+        do_b(6)
+        do_c(1)
+        part[8] = out_dot(s, w)
+        s, w = wait_dn(N_DN - 1)
+        do_a(8)
+        do_b(7)
+        do_c(2)
+        do_c(3)
+        part[9] = out_dot(s, w)
+        do_a(9)
+        do_b(8)
         do_c(4)
         do_c(5)
-        do_b(N_DN - 1)
-        for j in range(6, N_DN):
-            do_c(j)
-
-        for j in (N_DN, N_DN + 1):
-            local(wo_hbm.at[:, pl.ds(0, NB)], woring.at[j % WORING], wo_sem.at[j % WORING]).wait()
+        do_c(6)
+        do_b(9)
+        do_c(7)
+        do_c(8)
+        do_c(9)
+
         for j in range(N_DN - SB, N_DN):
             b_copy(j).wait_send()
 

time: 80.8 us -> 76.6 us (0.948)
  Pallas kernels: 78.7 us -> 74.5 us
    pallas_call x1, Pallas kernels: 78.7 us -> 74.5 us  [local_layer(): pl.pallas_call(body, out_shape=jax.ShapeDtypeStruct((TB, D), BF16), in_sp...]
where the time goes in v4:
time: 76.6 us; the launch traced here: 76.5 us
  Pallas kernels  74.5 us (97%)
  local copies, waits for them, and re-layouts  1.97 us (3%)
    pallas_call x1, Pallas kernels, local_layer(): pl.pallas_call(body, out_shape=jax.ShapeDtypeStruct((TB, D), BF16), in_sp...  74.5 us
    unnamed x1, local copies, waits for them, and re-layouts  1.97 us

profile of v4, /device:TPU:0, one launch (start us, length us, event | category | flops | bytes accessed | tf_op | source)
XLA Modules:
  0.0 76.5 jit_solution(4600027020466721304)
XLA Ops:
  0.0 74.5 %layer.1 = bf16[64,5120]{1,0:T(8,128)(2,1)} custom-call(bf16[64,5120]{1,0:T(8,128)(2,1)} %bitcast.10, f32[1,5120]{1,0:T(1,128)} %bitcast.11, f32[1,5120]{1,0:T(1,128)} %bitcast.12, f32[1,5120]{1,0:T(1,128)} %bitcast.13, f32[1,5120]{1,0:T(1,128)} %bitcast.14, bf16[10,5120,384]{2,1,0:T(8,128)(2,1)} %bitcast.8, bf16[1280,5120]{1,0:T(8,128)(2,1)} %wo_hbm.1, ...), custom_call_target="tpu_custom_call" | custom-call | flops 40299999232 | bytes 158000000 | tf_op jit(solution)/shard_map/layer/pallas_call | solution.py:403
  74.5 2.0 %copy.12 = bf16[1,64,5120]{2,1,0:T(8,128)(2,1)} copy(bf16[1,64,5120]{2,1,0:T(8,128)(2,1)} %bitcast.9) | data formatting | bytes 1310720

commit v5 on v3

--- a/solution.py
+++ b/solution.py
@@ -18,13 +18,14 @@
 NB = 512
 CTX = G * HD
 RING = 9
-WORING = 3
 SB = 4
 N_QKV = 8
 N_UP = FF // NB
 N_DN = D // NB
 UP0 = N_QKV
-DN0 = UP0 + N_UP
+WO0 = UP0 + N_UP
+N_WO = 3
+DN0 = WO0 + N_WO
 N_ITEMS = DN0 + N_DN
 NPIECE = 4
 PROWS = TB // NPIECE
@@ -36,8 +37,8 @@
 def body(x_hbm, ga_hbm, ba_hbm, gm_hbm, bm_hbm, wqkv_hbm, wo_hbm, wup_hbm, wdn_hbm, pos_hbm,
          out_hbm,
          x_own, abuf, ctx, norms, pos_v,
-         ring, woring, ra, sb, rb,
-         ring_sem, wo_sem, misc_sem, x_send, x_recv, c_send, c_recv, f_send, f_recv,
+         ring, ra, sb, rb,
+         ring_sem, misc_sem, x_send, x_recv, c_send, c_recv, f_send, f_recv,
          a_send, a_recv, b_send, b_recv, out_sem):
     t = lax.axis_index("tp")
     partner = t + 1 - 2 * lax.rem(t, 2)
@@ -71,17 +72,20 @@
     def issue(g):
         s = lax.rem(g, RING)
 
-        @pl.when(g < DN0)
+        @pl.when(g < WO0)
         def _():
             local(wup_hbm.at[:, cols(g - UP0)], ring.at[s], ring_sem.at[s]).start()
+
+        for q in range(N_WO):
+            @pl.when(g == WO0 + q)
+            def _(q=q):
+                for h in range(4 if q < 2 else 2):
+                    local(wo_hbm.at[:, pl.ds((4 * q + h) * NB, NB)], ring.at[(WO0 + q) % RING, pl.ds(h * CTX, CTX), :],
+                          ring_sem.at[(WO0 + q) % RING]).start()
 
         @pl.when(jnp.logical_and(g >= DN0, g < N_ITEMS))
         def _():
             local(wdn_hbm.at[:, cols(g - DN0)], ring.at[s], ring_sem.at[s]).start()
-
-    def issue_wo(j, c=None):
-        w = lax.rem(j, WORING)
-        local(wo_hbm.at[:, cols(j if c is None else c)], woring.at[w], wo_sem.at[w]).start()
 
     def wait_ring(g, n=NB):
         s = lax.rem(g, RING)
@@ -221,8 +225,6 @@
         qkv_last(far0)
         for p in (N_QKV - 2, N_QKV - 1):
             issue(jnp.int32(p + RING))
-        for j in range(WORING):
-            issue_wo(j)
 
         def rot(u):
             u = u.astype(F32)
@@ -300,64 +302,60 @@
             x_own[:, cols(j)] = (x_own[:, cols(j)].astype(F32) + (part[j, rows(t), :] + rb[j].astype(F32))).astype(BF16)
             out_copy(j).start()
 
-        def wait_dn(j):
-            s = wait_ring(j + DN0)
-            w = lax.rem(j, WORING)
-            local(wo_hbm.at[:, pl.ds(0, NB)], woring.at[w], wo_sem.at[w]).wait()
-            return s, w
-
-        def out_dot(s, w):
-            return (jnp.dot(ctx[...], woring[w], preferred_element_type=F32)
-                    + jnp.dot(abuf[...], ring[s], preferred_element_type=F32))
+        def out_dot(j, s):
+            return part[j] + jnp.dot(abuf[...], ring[s], preferred_element_type=F32)
 
         def refill(j):
             @pl.when(j + DN0 + RING < N_ITEMS)
             def _():
                 issue(j + DN0 + RING)
 
-        for g in (DN0 - 2, DN0 - 1):
+        for g in (WO0 - 2, WO0 - 1):
             issue(jnp.int32(g + RING))
 
-        def dn_pair(i, carry):
-            j = 2 * i
-            s0, w0 = wait_dn(j)
-            s1, w1 = wait_dn(j + 1)
-
-            @pl.when(i >= 1)
+        def wo_block(q, h, s):
+            part[4 * q + h] = jnp.dot(ctx[...], ring[s, pl.ds(h * CTX, CTX), :], preferred_element_type=F32)
+
+        def wo_step(q, carry):
+            s = wait_ring(WO0 + q)
+            for h in range(4):
+                wo_block(q, h, s)
+            issue(WO0 + q + RING)
+            return carry
+
+        lax.fori_loop(0, N_WO - 1, wo_step, 0)
+        s = (DN0 - 1) % RING
+        local(wup_hbm.at[pl.ds(0, 2 * CTX), pl.ds(0, NB)], ring.at[s, pl.ds(0, 2 * CTX), :], ring_sem.at[s]).wait()
+        for h in range(2):
+            wo_block(N_WO - 1, h, s)
+        issue(jnp.int32(DN0 - 1 + RING))
+
+        def dn_step(j, carry):
+            s = wait_ring(j + DN0)
+
+            @pl.when(j >= 1)
             def _():
                 do_a(j - 1)
-                refill(j - 2)
                 refill(j - 1)
-                issue_wo(j + 2, jnp.minimum(j + 2, N_DN - 1))
+
+            @pl.when(j >= 2)
+            def _():
                 do_b(j - 2)
 
-            @pl.when(i >= 2)
-            def _():
-                do_b(j - 3)
-
-            @pl.when(i >= 3)
-            def _():
-                do_c(j - 6)
-                do_c(j - 5)
-            part[j] = out_dot(s0, w0)
-            issue_wo(j + 3, jnp.minimum(j + 3, N_DN - 1))
-            part[j + 1] = out_dot(s1, w1)
-            do_a(j)
-            return carry
-
-        N_PAIR = 5
-        lax.fori_loop(0, N_PAIR, dn_pair, 0)
+            @pl.when(j >= 4)
+            def _():
+                do_c(j - 4)
+            part[j] = out_dot(j, s)
+            return carry
+
+        lax.fori_loop(0, N_DN, dn_step, 0)
         do_a(N_DN - 1)
-        do_b(N_DN - 3)
         do_b(N_DN - 2)
-        do_c(4)
-        do_c(5)
+        do_c(N_DN - 4)
         do_b(N_DN - 1)
-        for j in range(6, N_DN):
+        for j in range(N_DN - 3, N_DN):
             do_c(j)
 
-        for j in (N_DN, N_DN + 1):
-            local(wo_hbm.at[:, pl.ds(0, NB)], woring.at[j % WORING], wo_sem.at[j % WORING]).wait()
         for j in range(N_DN - SB, N_DN):
             b_copy(j).wait_send()
 
@@ -393,11 +391,10 @@
                 pltpu.VMEM((4, D), F32),
                 pltpu.VMEM((1, T), jnp.int32),
                 pltpu.VMEM((RING, D, NB), BF16),
-                pltpu.VMEM((WORING, CTX, NB), BF16),
                 pltpu.VMEM((RA, 2, TB, NB), F32),
                 pltpu.VMEM((SB, TB, NB), BF16),
                 pltpu.VMEM((N_DN, TB, NB), BF16),
-                dma((RING,)), dma((WORING,)), dma((6,)), dma((1,)), dma((1,)), dma((NPIECE,)), dma((NPIECE,)),
+                dma((RING,)), dma((6,)), dma((1,)), dma((1,)), dma((NPIECE,)), dma((NPIECE,)),
                 dma((NPIECE,)), dma((NPIECE,)), dma((N_DN, 2)), dma((N_DN, 2)), dma((N_DN,)), dma((N_DN,)), dma((N_DN,)),
             ],
             compiler_params=pltpu.CompilerParams(collective_id=0, has_side_effects=True, vmem_limit_bytes=67043328),

time: 80.8 us -> 71.7 us (0.89)
  Pallas kernels: 78.7 us -> 69.6 us
    pallas_call x1, Pallas kernels: 78.7 us -> 69.6 us  [local_layer(): pl.pallas_call(body, out_shape=jax.ShapeDtypeStruct((TB, D), BF16), in_sp...]
where the time goes in v5:
time: 71.7 us; the launch traced here: 71.5 us
  Pallas kernels  69.6 us (97%)
  local copies, waits for them, and re-layouts  1.97 us (3%)
    pallas_call x1, Pallas kernels, local_layer(): pl.pallas_call(body, out_shape=jax.ShapeDtypeStruct((TB, D), BF16), in_sp...  69.6 us
    unnamed x1, local copies, waits for them, and re-layouts  1.97 us

profile of v5, /device:TPU:0, one launch (start us, length us, event | category | flops | bytes accessed | tf_op | source)
XLA Modules:
  0.0 71.5 jit_solution(13818816537441227205)
XLA Ops:
  0.0 69.6 %layer.1 = bf16[64,5120]{1,0:T(8,128)(2,1)} custom-call(bf16[64,5120]{1,0:T(8,128)(2,1)} %bitcast.10, f32[1,5120]{1,0:T(1,128)} %bitcast.11, f32[1,5120]{1,0:T(1,128)} %bitcast.12, f32[1,5120]{1,0:T(1,128)} %bitcast.13, f32[1,5120]{1,0:T(1,128)} %bitcast.14, bf16[10,5120,384]{2,1,0:T(8,128)(2,1)} %bitcast.8, bf16[1280,5120]{1,0:T(8,128)(2,1)} %wo_hbm.1, ...), custom_call_target="tpu_custom_call" | custom-call | flops 40299999232 | bytes 158000000 | tf_op jit(solution)/shard_map/layer/pallas_call | solution.py:382
  69.6 2.0 %copy.12 = bf16[1,64,5120]{2,1,0:T(8,128)(2,1)} copy(bf16[1,64,5120]{2,1,0:T(8,128)(2,1)} %bitcast.9) | data formatting | bytes 1310720

commit v6 on v5

--- a/solution.py
+++ b/solution.py
@@ -282,14 +282,16 @@
             for i in range(2):
                 a_copy(j, i).start()
 
-        def do_b(j):
+        def do_b(j, late=False):
             for i in range(2):
                 a_copy(j, i).wait_recv()
             r = lax.rem(j, RA)
-
-            @pl.when(j >= SB)
-            def _():
+            if late:
                 b_copy(j - SB).wait_send()
+            else:
+                @pl.when(j >= SB)
+                def _():
+                    b_copy(j - SB).wait_send()
             sb[lax.rem(j, SB)] = (part[j, rows(cross), :] + ra[r, 1]).astype(BF16)
             b_copy(j).start()
             part[j, rows(t), :] = part[j, rows(t), :] + ra[r, 0]
@@ -348,24 +350,38 @@
             part[j] = out_dot(j, s)
             return carry
 
-        lax.fori_loop(0, N_DN, dn_step, 0)
+        def dn_late(j, carry):
+            s = wait_ring(j + DN0)
+            do_a(j - 1)
+            do_b(j - 2, late=True)
+            do_c(j - 4)
+            part[j] = out_dot(j, s)
+            return carry
+
+        lax.fori_loop(0, SB + 2, dn_step, 0)
+        lax.fori_loop(SB + 2, N_DN, dn_late, 0)
         do_a(N_DN - 1)
-        do_b(N_DN - 2)
+        do_b(N_DN - 2, late=True)
         do_c(N_DN - 4)
-        do_b(N_DN - 1)
-        for j in range(N_DN - 3, N_DN):
-            do_c(j)
-
+        do_c(N_DN - 3)
+        do_b(N_DN - 1, late=True)
+
+        def sent(j, carry):
+            for i in range(2):
+                a_copy(j, i).wait_send()
+            return carry
+
+        def stored(j, carry):
+            out_copy(j).wait()
+            return carry
+
+        lax.fori_loop(0, N_DN, sent, 0)
+        lax.fori_loop(0, N_DN - 3, stored, 0)
+        do_c(N_DN - 2)
         for j in range(N_DN - SB, N_DN):
             b_copy(j).wait_send()
-
-        def drain(j, carry):
-            for i in range(2):
-                a_copy(j, i).wait_send()
-            out_copy(j).wait()
-            return carry
-
-        lax.fori_loop(0, N_DN, drain, 0)
+        do_c(N_DN - 1)
+        lax.fori_loop(N_DN - 3, N_DN, stored, 0)
 
     pl.run_scoped(front, pltpu.VMEM((T, D), BF16), pltpu.VMEM((N_QKV, T, NB), BF16),
                   pltpu.VMEM((T, HD), F32), pltpu.VMEM((T, HD), F32), pltpu.VMEM((T, NB), F32))

time: 71.7 us -> 71.6 us (level)
  no operation moved by 1% of the time
where the time goes in v6:
time: 71.6 us; the launch traced here: 71.5 us
  Pallas kernels  69.5 us (97%)
  local copies, waits for them, and re-layouts  1.97 us (3%)
    pallas_call x1, Pallas kernels, local_layer(): pl.pallas_call(body, out_shape=jax.ShapeDtypeStruct((TB, D), BF16), in_sp...  69.5 us
    unnamed x1, local copies, waits for them, and re-layouts  1.97 us

profile of v6, /device:TPU:0, one launch (start us, length us, event | category | flops | bytes accessed | tf_op | source)
XLA Modules:
  0.0 71.5 jit_solution(7833541426736568887)
XLA Ops:
  0.0 69.5 %layer.1 = bf16[64,5120]{1,0:T(8,128)(2,1)} custom-call(bf16[64,5120]{1,0:T(8,128)(2,1)} %bitcast.10, f32[1,5120]{1,0:T(1,128)} %bitcast.11, f32[1,5120]{1,0:T(1,128)} %bitcast.12, f32[1,5120]{1,0:T(1,128)} %bitcast.13, f32[1,5120]{1,0:T(1,128)} %bitcast.14, bf16[10,5120,384]{2,1,0:T(8,128)(2,1)} %bitcast.8, bf16[1280,5120]{1,0:T(8,128)(2,1)} %wo_hbm.1, ...), custom_call_target="tpu_custom_call" | custom-call | flops 40299999232 | bytes 158000000 | tf_op jit(solution)/shard_map/layer/pallas_call | solution.py:398
  69.5 2.0 %copy.12 = bf16[1,64,5120]{2,1,0:T(8,128)(2,1)} copy(bf16[1,64,5120]{2,1,0:T(8,128)(2,1)} %bitcast.9) | data formatting | bytes 1310720

commit v7 on v6

--- a/solution.py
+++ b/solution.py
@@ -271,20 +271,19 @@
         gelu_store(acc[...], N_UP - 1)
 
     def back(part):
-        def a_copy(j, i):
-            blk = partner if i == 0 else diag
-            return remote(part.at[j, rows(blk)], ra.at[lax.rem(j, RA), i], a_send.at[j, i], a_recv.at[j, i], partner)
+        chip, core = t // 2, lax.rem(t, 2)
+
+        def a_copy(j):
+            return remote(part.at[j, :, 1 - core], ra.at[lax.rem(j, RA)], a_send.at[j], a_recv.at[j], partner)
 
         def b_copy(j):
-            return remote(sb.at[lax.rem(j, SB)], rb.at[j], b_send.at[j], b_recv.at[j], cross)
+            return remote(sb.at[lax.rem(j, SB)], rb.at[j], b_send.at[lax.rem(j, SB)], b_recv.at[j], cross)
 
         def do_a(j):
-            for i in range(2):
-                a_copy(j, i).start()
+            a_copy(j).start()
 
         def do_b(j, late=False):
-            for i in range(2):
-                a_copy(j, i).wait_recv()
+            a_copy(j).wait_recv()
             r = lax.rem(j, RA)
             if late:
                 b_copy(j - SB).wait_send()
@@ -292,20 +291,20 @@
                 @pl.when(j >= SB)
                 def _():
                     b_copy(j - SB).wait_send()
-            sb[lax.rem(j, SB)] = (part[j, rows(cross), :] + ra[r, 1]).astype(BF16)
+            sb[lax.rem(j, SB)] = (part[j, 1 - chip, core] + ra[r, 1 - chip]).astype(BF16)
             b_copy(j).start()
-            part[j, rows(t), :] = part[j, rows(t), :] + ra[r, 0]
+            part[j, chip, core] = part[j, chip, core] + ra[r, chip]
 
         def out_copy(j):
             return local(x_own.at[:, cols(j)], out_hbm.at[:, cols(j)], out_sem.at[j])
 
         def do_c(j):
             b_copy(j).wait_recv()
-            x_own[:, cols(j)] = (x_own[:, cols(j)].astype(F32) + (part[j, rows(t), :] + rb[j].astype(F32))).astype(BF16)
+            x_own[:, cols(j)] = (x_own[:, cols(j)].astype(F32) + (part[j, chip, core] + rb[j].astype(F32))).astype(BF16)
             out_copy(j).start()
 
         def out_dot(j, s):
-            return part[j] + jnp.dot(abuf[...], ring[s], preferred_element_type=F32)
+            return part[j] + jnp.dot(abuf[...], ring[s], preferred_element_type=F32).reshape(2, 2, TB, NB)
 
         def refill(j):
             @pl.when(j + DN0 + RING < N_ITEMS)
@@ -316,7 +315,7 @@
             issue(jnp.int32(g + RING))
 
         def wo_block(q, h, s):
-            part[4 * q + h] = jnp.dot(ctx[...], ring[s, pl.ds(h * CTX, CTX), :], preferred_element_type=F32)
+            part[4 * q + h] = jnp.dot(ctx[...], ring[s, pl.ds(h * CTX, CTX), :], preferred_element_type=F32).reshape(2, 2, TB, NB)
 
         def wo_step(q, carry):
             s = wait_ring(WO0 + q)
@@ -367,8 +366,7 @@
         do_b(N_DN - 1, late=True)
 
         def sent(j, carry):
-            for i in range(2):
-                a_copy(j, i).wait_send()
+            a_copy(j).wait_send()
             return carry
 
         def stored(j, carry):
@@ -387,7 +385,7 @@
                   pltpu.VMEM((T, HD), F32), pltpu.VMEM((T, HD), F32), pltpu.VMEM((T, NB), F32))
     for c in to_cross + [to_partner]:
         c.wait_send()
-    pl.run_scoped(back, pltpu.VMEM((N_DN, T, NB), F32))
+    pl.run_scoped(back, pltpu.VMEM((N_DN, 2, 2, TB, NB), F32))
 
 
 def solution(mesh):
@@ -411,7 +409,7 @@
                 pltpu.VMEM((SB, TB, NB), BF16),
                 pltpu.VMEM((N_DN, TB, NB), BF16),
                 dma((RING,)), dma((6,)), dma((1,)), dma((1,)), dma((NPIECE,)), dma((NPIECE,)),
-                dma((NPIECE,)), dma((NPIECE,)), dma((N_DN, 2)), dma((N_DN, 2)), dma((N_DN,)), dma((N_DN,)), dma((N_DN,)),
+                dma((NPIECE,)), dma((NPIECE,)), dma((N_DN,)), dma((N_DN,)), dma((SB,)), dma((N_DN,)), dma((N_DN,)),
             ],
             compiler_params=pltpu.CompilerParams(collective_id=0, has_side_effects=True, vmem_limit_bytes=67043328),
             cost_estimate=pl.CostEstimate(flops=40_300_000_000, bytes_accessed=158_000_000, transcendentals=2_000_000),

time: 71.6 us -> 71.4 us (level)
  no operation moved by 1% of the time
where the time goes in v7:
time: 71.4 us; the launch traced here: 71.2 us
  Pallas kernels  69.3 us (97%)
  local copies, waits for them, and re-layouts  1.97 us (3%)
    pallas_call x1, Pallas kernels, local_layer(): pl.pallas_call(body, out_shape=jax.ShapeDtypeStruct((TB, D), BF16), in_sp...  69.3 us
    unnamed x1, local copies, waits for them, and re-layouts  1.97 us

profile of v7, /device:TPU:0, one launch (start us, length us, event | category | flops | bytes accessed | tf_op | source)
XLA Modules:
  0.0 71.2 jit_solution(7224372554501214486)
XLA Ops:
  0.0 69.3 %layer.1 = bf16[64,5120]{1,0:T(8,128)(2,1)} custom-call(bf16[64,5120]{1,0:T(8,128)(2,1)} %bitcast.10, f32[1,5120]{1,0:T(1,128)} %bitcast.11, f32[1,5120]{1,0:T(1,128)} %bitcast.12, f32[1,5120]{1,0:T(1,128)} %bitcast.13, f32[1,5120]{1,0:T(1,128)} %bitcast.14, bf16[10,5120,384]{2,1,0:T(8,128)(2,1)} %bitcast.8, bf16[1280,5120]{1,0:T(8,128)(2,1)} %wo_hbm.1, ...), custom_call_target="tpu_custom_call" | custom-call | flops 40299999232 | bytes 158000000 | tf_op jit(solution)/shard_map/layer/pallas_call | solution.py:396
  69.3 2.0 %copy.12 = bf16[1,64,5120]{2,1,0:T(8,128)(2,1)} copy(bf16[1,64,5120]{2,1,0:T(8,128)(2,1)} %bitcast.9) | data formatting | bytes 1310720
